TPU v7x, 32 devices: a whole 2x2x4 slice. The times are simulated.
32 devices in a mesh: rows: 8 (over z, x), cols: 4 (over y, core).
Axes of the slice: x: 2, y: 2, z: 4, core: 2. Of those that a mesh axis runs over, the one named last changes fastest.
Arguments:
- vectors: bfloat16 [1024, 32768], P(None, 'rows'), may hold values from -0.4 to 0.4
- integrals: bfloat16 [2, 256, 32768], P(None, 'cols', 'rows'), may hold values from -8 to 72
- pivots: int32 [2, 256], replicated, may hold values from 0 to 32767, as said below
Outputs:
- new_vectors: float32 [2, 256, 32768], P(None, 'cols', 'rows')
Inputs may be any that keep to these rules, and one draw needn't show every extreme that they name: The 2 x 256 entries are distinct shell-pair rows. In each panel the rows of one index of rows (an aligned block of 4096) hold at most 64 pivots, and some block holds exactly 64.
All inputs are finite; a program needn't handle non-finite values.
Results may differ from a plain program's by a relative error of at most 0.00036.
Values may be sent and summed in bfloat16 or wider, within the bound.
No kernel may reach another device: no remote copies, remote signals or barrier semaphores. Data moves between devices by JAX's collectives and lax.ppermute only.
A program may use at most 64 MiB of HBM per device.

v0:
```python
import jax
import jax.numpy as jnp
from jax import lax
from jax.sharding import PartitionSpec as P

PW = 256
PANELS = 2


def select_matrix(row_count, targets):
    return (jnp.arange(row_count, dtype=jnp.int32)[:, None] == targets[None, :]).astype(
        jnp.bfloat16
    )


def transposed_product(left, right):
    return lax.dot_general(
        left, right, (((0,), (0,)), ((), ())), preferred_element_type=jnp.float32
    )


def solve_block(lower_factor, residual):
    return jax.scipy.linalg.solve_triangular(lower_factor, residual, lower=True)


def per_device(vectors, integrals, pivots):
    row_count = vectors.shape[1]
    block_cols = integrals.shape[1]
    owners = lax.axis_size("rows")
    owner_index = lax.axis_index("rows")
    owner_start = owner_index * row_count
    col_start = lax.axis_index("cols") * block_cols
    factors = [vectors]
    results = []
    for panel in range(PANELS):
        pivot_row = pivots[panel]
        local_targets = pivot_row - owner_start
        slot_count = 2 * PW // owners
        owner_of = pivot_row // row_count
        order = jnp.arange(PW, dtype=jnp.int32)
        earlier = (owner_of[None, :] == owner_of[:, None]) & (order[None, :] < order[:, None])
        slot_rank = jnp.sum(earlier.astype(jnp.int32), axis=1)
        mine = owner_of == owner_index
        slot_pick = (
            (slot_rank[:, None] == jnp.arange(slot_count, dtype=jnp.int32)[None, :]) & mine[:, None]
        ).astype(jnp.bfloat16)
        slot_select = jnp.dot(
            select_matrix(row_count, local_targets), slot_pick, preferred_element_type=jnp.float32
        ).astype(jnp.bfloat16)
        sending = jnp.concatenate(
            [
                jnp.dot(factor, slot_select, preferred_element_type=jnp.float32)
                for factor in factors
            ],
            axis=0,
        ).astype(jnp.bfloat16)
        targets = lax.dynamic_slice_in_dim(owner_of * slot_count + slot_rank, col_start, block_cols)
        receive_pick = select_matrix(owners * slot_count, targets)
        picked = jnp.dot(
            lax.all_gather(sending, "rows", axis=1, tiled=True),
            receive_pick,
            preferred_element_type=jnp.float32,
        ).astype(jnp.bfloat16)
        residual = integrals[panel].astype(jnp.float32)
        offset = 0
        for factor in factors:
            residual = residual - transposed_product(
                picked[offset : offset + factor.shape[0]], factor
            )
            offset = offset + factor.shape[0]
        every_pivot = select_matrix(row_count, local_targets).astype(jnp.float32)
        contribution = jnp.dot(residual, every_pivot, precision=lax.Precision.HIGHEST)
        placed = lax.dynamic_update_slice(
            jnp.zeros((PW, PW), jnp.float32), contribution, (col_start, 0)
        )
        block = lax.psum(placed, ("rows", "cols"))
        lower_factor = jnp.linalg.cholesky(0.5 * (block + block.T))
        whole = lax.all_gather(residual, "cols", axis=0, tiled=True)
        solved = solve_block(lower_factor, whole)
        fresh = lax.dynamic_slice_in_dim(solved, col_start, block_cols, 0)
        if panel + 1 < PANELS:
            factors.append(solved.astype(jnp.bfloat16))
        results.append(fresh)
    return jnp.stack(results)


def solution(mesh):
    placed = (P(None, "rows"), P(None, "cols", "rows"), P())
    return jax.shard_map(
        per_device, mesh=mesh, in_specs=placed, out_specs=P(None, "cols", "rows"), check_vma=False
    )
```

profile of v0, /device:TPU:0, one launch (start us, length us, event | category | flops | bytes accessed | tf_op | source)
XLA Modules:
  0.0 519.9 jit_solution(4560592978291593466)
XLA Ops:
  7.5 7.5 %fusion.14 = bf16[1024,64]{0,1:T(8,128)(2,1)} fusion(bf16[1024,4096]{1,0:T(8,128)(2,1)} %param.6, s32[256]{0:T(256)S(1)} %bitcast.98, s32[256]{0:T(256)S(1)} %convert_reduce_fusion.1, pred[256]{0:T(512)(128)(4,1)S(1)} %get-tuple-element.65), kind=kOutput, calls=%fused_computation.36 | convolution fusion | flops 672497664 | bytes 8521984 | tf_op jit(solution)/shard_map/dot_general | solution.py:52
  15.2 43.0 %all-gather.5.cloned.1.call-done = bf16[1024,512]{0,1:T(8,128)(2,1)} async-done(((bf16[1024,64]{0,1:T(8,128)(2,1)}), bf16[1024,512]{0,1:T(8,128)(2,1)}) %all-gather.5.cloned.1.call-update) | async-done | bytes 1048592 | tf_op jit(solution)/shard_map/all_gather | solution.py:60
  58.2 5.9 %convolution_subtract_fusion.4 = f32[64,4096]{1,0:T(8,128)S(1)} fusion(bf16[1024,4096]{1,0:T(8,128)(2,1)} %param.6, bf16[1024,512]{0,1:T(8,128)(2,1)} %all-gather.5.cloned.1.call-done, bf16[2,64,4096]{2,1,0:T(8,128)(2,1)S(1)} %copy-done.6, s32[64]{0:T(128)S(1)} %dynamic_slice.12), kind=kOutput, calls=%fused_computation.12 | convolution fusion | flops 604602368 | bytes 11010304 | tf_op jit(solution)/shard_map/dot_general | solution.py:17
  64.1 1.7 fusion.15
  68.7 6.1 %fusion.13 = bf16[1024,64]{0,1:T(8,128)(2,1)S(1)} fusion(bf16[4096,64]{0,1:T(8,128)(2,1)S(1)} %convolution_convert_fusion.1, bf16[1024,4096]{1,0:T(8,128)(2,1)} %param.6), kind=kOutput, calls=%fused_computation.35 | convolution fusion | flops 536936448 | bytes 9043968 | tf_op jit(solution)/shard_map/dot_general | solution.py:52
  74.7 117.2 %all-reduce.4.cloned.1.call-done = f32[256,256]{1,0:T(8,128)} async-done(((f32[256,256]{1,0:T(8,128)}), f32[256,256]{1,0:T(8,128)}) %all-reduce.4.cloned.1.call-update) | async-done | bytes 262160 | tf_op jit(solution)/shard_map/psum | solution.py:76
  194.2 11.7 %cholesky.130 = f32[128,128]{1,0:T(8,128)S(1)} custom-call(f32[128,128]{1,0:T(8,128)S(1)} %cholesky.194), custom_call_target="Cholesky" | custom-call | tf_op jit(solution)/shard_map/jit(cholesky)/cholesky | solution.py:77
  206.0 9.8 %custom-call.13 = f32[1,128,128]{1,2,0:T(8,128)S(1)} custom-call(f32[1,128,128]{2,1,0:T(8,128)S(1)} %get-tuple-element.54), custom_call_target="InvertDiagBlocksLowerTriangular" | custom-call | tf_op jit(solution)/shard_map/jit(cholesky)/cholesky | solution.py:77
  216.3 11.9 %cholesky.147 = f32[128,128]{1,0:T(8,128)S(1)} custom-call(f32[128,128]{1,0:T(8,128)S(1)} %convolution_subtract_fusion.6), custom_call_target="Cholesky" | custom-call | tf_op jit(solution)/shard_map/jit(cholesky)/cholesky | solution.py:77
  231.0 4.1 while.4
  231.7 1.4 bitcast_dynamic-update-slice_fusion.4
  233.7 1.4 bitcast_dynamic-update-slice_fusion.4
  235.1 19.7 %custom-call.14 = f32[2,128,128]{1,2,0:T(8,128)S(1)} custom-call(f32[2,128,128]{2,1,0:T(8,128)S(1)} %get-tuple-element.21), custom_call_target="InvertDiagBlocksLowerTriangular" | custom-call | tf_op jit(solution)/shard_map/jit(_solve_triangular)/triangular_solve | solution.py:23
  254.8 3.6 fusion.5
  258.5 1.9 convolution_subtract_fusion.1
  260.4 1.9 fusion.42
  264.6 40.9 %all-gather.9.cloned.1.call-done = bf16[1280,512]{0,1:T(8,128)(2,1)} async-done(((bf16[1280,64]{0,1:T(8,128)(2,1)}), bf16[1280,512]{0,1:T(8,128)(2,1)}) %all-gather.9.cloned.1.call-update) | async-done | bytes 1310736 | tf_op jit(solution)/shard_map/all_gather | solution.py:60
  305.5 1.7 convolution_convert_fusion.2
  307.2 5.1 convolution_subtract_fusion.3
  312.9 1.7 fusion.16
  316.0 124.8 %all-reduce.6.cloned.1.call-done = f32[256,256]{1,0:T(8,128)} async-done(((f32[256,256]{1,0:T(8,128)}), f32[256,256]{1,0:T(8,128)}) %all-reduce.6.cloned.1.call-update) | async-done | bytes 262160 | tf_op jit(solution)/shard_map/psum | solution.py:76
  443.3 11.7 %cholesky.164 = f32[128,128]{1,0:T(8,128)S(1)} custom-call(f32[128,128]{1,0:T(8,128)S(1)} %cholesky.197), custom_call_target="Cholesky" | custom-call | tf_op jit(solution)/shard_map/jit(cholesky)/cholesky | solution.py:77
  455.0 9.8 %custom-call.15 = f32[1,128,128]{1,2,0:T(8,128)S(1)} custom-call(f32[1,128,128]{2,1,0:T(8,128)S(1)} %get-tuple-element.50), custom_call_target="InvertDiagBlocksLowerTriangular" | custom-call | tf_op jit(solution)/shard_map/jit(cholesky)/cholesky | solution.py:77
  465.4 11.7 %cholesky.181 = f32[128,128]{1,0:T(8,128)S(1)} custom-call(f32[128,128]{1,0:T(8,128)S(1)} %convolution_subtract_fusion.5), custom_call_target="Cholesky" | custom-call | tf_op jit(solution)/shard_map/jit(cholesky)/cholesky | solution.py:77
  479.7 4.1 while.5
  480.5 1.4 bitcast_dynamic-update-slice_fusion.5
  482.5 1.4 bitcast_dynamic-update-slice_fusion.5
  483.9 19.7 %custom-call.16 = f32[2,128,128]{1,2,0:T(8,128)S(1)} custom-call(f32[2,128,128]{2,1,0:T(8,128)S(1)} %get-tuple-element.22), custom_call_target="InvertDiagBlocksLowerTriangular" | custom-call | tf_op jit(solution)/shard_map/jit(_solve_triangular)/triangular_solve | solution.py:23
  503.6 3.6 fusion.3
  507.2 1.9 convolution_subtract_fusion
  509.2 1.9 fusion.38
  511.3 1.5 pad_maximum_fusion.1
  (90 shorter events, 19.4 us)
Async XLA Ops:
  6.5 51.7 %all-gather.5.cloned.1.call-start = ((), (), s32[]{:S(2)}) async-start(), calls=%async_computation | async-start | bytes 1179648 | tf_op jit(solution)/shard_map/all_gather | solution.py:60
  7.5 50.7 %copy-start.6 = (bf16[2,64,4096]{2,1,0:T(8,128)(2,1)S(1)}, bf16[2,64,4096]{2,1,0:T(8,128)(2,1)}, u32[]{:S(2)}) copy-start(bf16[2,64,4096]{2,1,0:T(8,128)(2,1)} %param.7) | copy-start | bytes 3145732
  15.0 176.9 %all-reduce.4.cloned.1.call-start = ((), (), s32[]{:S(2)}) async-start(), calls=%async_computation.1 | async-start | bytes 524288 | tf_op jit(solution)/shard_map/psum | solution.py:76
  64.1 2.5 copy-start.5
  65.8 0.7 copy-start.8
  66.5 188.3 %all-gather.7.cloned.1.call-start = ((), (), s32[]{:S(2)}) async-start(), calls=%async_computation.2 | async-start | bytes 5242880 | tf_op jit(solution)/shard_map/all_gather | solution.py:78
  67.3 238.2 %all-gather.9.cloned.1.call-start = ((), (), s32[]{:S(2)}) async-start(), calls=%async_computation.3 | async-start | bytes 1474560 | tf_op jit(solution)/shard_map/all_gather | solution.py:60
  254.8 3.7 copy-start.2
  262.4 1.3 copy-start
  263.7 43.5 %copy-start.7 = (bf16[2,64,4096]{2,1,0:T(8,128)(2,1)S(1)}, bf16[2,64,4096]{2,1,0:T(8,128)(2,1)}, u32[]{:S(2)}) copy-start(bf16[2,64,4096]{2,1,0:T(8,128)(2,1)} %param.7) | copy-start | bytes 3145732
  264.4 176.4 %all-reduce.6.cloned.1.call-start = ((), (), s32[]{:S(2)}) async-start(), calls=%async_computation.4 | async-start | bytes 524288 | tf_op jit(solution)/shard_map/psum | solution.py:76
  307.2 5.2 copy-start.1
  312.9 2.9 copy-start.4
  314.6 0.7 copy-start.9
  315.3 188.3 %all-gather.11.cloned.1.call-start = ((), (), s32[]{:S(2)}) async-start(), calls=%async_computation.5 | async-start | bytes 5242880 | tf_op jit(solution)/shard_map/all_gather | solution.py:78
  503.6 3.7 copy-start.3
Sparse Core Ops, SparseCore 0:
  15.2 42.9 all-gather.4
  66.6 125.2 all-reduce.3
  193.5 33.7 all-gather.6
  264.5 40.8 all-gather.8
  315.4 125.3 all-reduce.5
  442.3 33.6 all-gather.10
where the time goes:
time: 525 us; the launch traced here: 520 us
  waiting for transfers between devices  327 us (62%)
  other arithmetic  115 us (22%)
  matrix products  47.8 us (9%)
  between operations  16.7 us (3%)
  local copies, waits for them, and re-layouts  12.8 us (2%)
    psum x2, waiting for transfers between devices, per_device(): block = lax.psum(placed, ('rows', 'cols'))  242 us
    all_gather x2, waiting for transfers between devices, per_device(): lax.all_gather(sending, 'rows', axis=1, tiled=True)  83.9 us
    another operation x14, other arithmetic, per_device(): lower_factor = jnp.linalg.cholesky(0.5 * (block + block.T))  69.4 us
    another operation x5, other arithmetic, solve_block(): return jax.scipy.linalg.solve_triangular(lower_factor, residual, lower=True)  39.4 us
    another operation x6, matrix products, solve_block(): return jax.scipy.linalg.solve_triangular(lower_factor, residual, lower=True)  15 us
    dot_general x3, matrix products, per_device(): jnp.dot(factor, slot_select, preferred_element_type=jnp.float32)  14.4 us
    dot_general x3, matrix products, transposed_product(): lax.dot_general(left, right, (((0,), (0,)), ((), ())), preferred_element_...  11.5 us
  transfers between devices with their start and end apart: 6, of which 4 were waited for; matrix products, arithmetic and copies ran while one was open for 25% of the time, Pallas kernels for 0%

commit v1 on v0

--- a/solution.py
+++ b/solution.py
@@ -73,7 +73,7 @@
         placed = lax.dynamic_update_slice(
             jnp.zeros((PW, PW), jnp.float32), contribution, (col_start, 0)
         )
-        block = lax.psum(placed, ("rows", "cols"))
+        block = lax.psum(lax.psum(placed, "cols"), "rows")
         lower_factor = jnp.linalg.cholesky(0.5 * (block + block.T))
         whole = lax.all_gather(residual, "cols", axis=0, tiled=True)
         solved = solve_block(lower_factor, whole)

time: 525 us -> 486 us (0.926)
  waiting for transfers between devices: 327 us -> 287 us
    psum x2 -> x4, waiting for transfers between devices: 242 us -> 202 us  [per_device(): block = lax.psum(lax.psum(placed, 'cols'), 'rows')]
  transfers between devices with their start and end apart: 6 -> 8, of which waited for: 4 -> 6; matrix products, arithmetic and copies ran while one was open for 25% -> 27% of each run, Pallas kernels for 0% -> 0%
where the time goes in v1:
time: 486 us; the launch traced here: 480 us
  waiting for transfers between devices  287 us (59%)
  other arithmetic  115 us (24%)
  matrix products  47.8 us (10%)
  between operations  16.7 us (3%)
  local copies, waits for them, and re-layouts  12.8 us (3%)
    psum x4, waiting for transfers between devices, per_device(): block = lax.psum(lax.psum(placed, 'cols'), 'rows')  202 us
    all_gather x2, waiting for transfers between devices, per_device(): lax.all_gather(sending, 'rows', axis=1, tiled=True)  84 us
    another operation x14, other arithmetic, per_device(): lower_factor = jnp.linalg.cholesky(0.5 * (block + block.T))  69.5 us
    another operation x5, other arithmetic, solve_block(): return jax.scipy.linalg.solve_triangular(lower_factor, residual, lower=True)  39.4 us
    another operation x6, matrix products, solve_block(): return jax.scipy.linalg.solve_triangular(lower_factor, residual, lower=True)  15 us
    dot_general x3, matrix products, per_device(): jnp.dot(factor, slot_select, preferred_element_type=jnp.float32)  14.3 us
    dot_general x3, matrix products, transposed_product(): lax.dot_general(left, right, (((0,), (0,)), ((), ())), preferred_element_...  11.5 us
  transfers between devices with their start and end apart: 8, of which 6 were waited for; matrix products, arithmetic and copies ran while one was open for 27% of the time, Pallas kernels for 0%

profile of v1, /device:TPU:0, one launch (start us, length us, event | category | flops | bytes accessed | tf_op | source)
XLA Modules:
  0.0 480.3 jit_solution(2782597846670198541)
XLA Ops:
  7.5 7.5 %fusion.14 = bf16[1024,64]{0,1:T(8,128)(2,1)} fusion(bf16[1024,4096]{1,0:T(8,128)(2,1)} %param.6, s32[256]{0:T(256)S(1)} %bitcast.98, s32[256]{0:T(256)S(1)} %convert_reduce_fusion.1, pred[256]{0:T(512)(128)(4,1)S(1)} %get-tuple-element.65), kind=kOutput, calls=%fused_computation.36 | convolution fusion | flops 672497664 | bytes 8521984 | tf_op jit(solution)/shard_map/dot_general | solution.py:52
  15.2 43.0 %all-gather.5.cloned.1.call-done = bf16[1024,512]{0,1:T(8,128)(2,1)} async-done(((bf16[1024,64]{0,1:T(8,128)(2,1)}), bf16[1024,512]{0,1:T(8,128)(2,1)}) %all-gather.5.cloned.1.call-update) | async-done | bytes 1048592 | tf_op jit(solution)/shard_map/all_gather | solution.py:60
  58.2 5.9 %convolution_subtract_fusion.4 = f32[64,4096]{1,0:T(8,128)S(1)} fusion(bf16[1024,4096]{1,0:T(8,128)(2,1)} %param.6, bf16[1024,512]{0,1:T(8,128)(2,1)} %all-gather.5.cloned.1.call-done, bf16[2,64,4096]{2,1,0:T(8,128)(2,1)S(1)} %copy-done.6, s32[64]{0:T(128)S(1)} %dynamic_slice.12), kind=kOutput, calls=%fused_computation.12 | convolution fusion | flops 604602368 | bytes 11010304 | tf_op jit(solution)/shard_map/dot_general | solution.py:17
  64.1 1.7 fusion.15
  66.5 31.1 %all-reduce.6.cloned.1.call-done = f32[256,256]{1,0:T(8,128)} async-done(((f32[256,256]{1,0:T(8,128)}), f32[256,256]{1,0:T(8,128)}) %all-reduce.6.cloned.1.call-update) | async-done | bytes 262160 | tf_op jit(solution)/shard_map/psum | solution.py:76
  99.6 6.0 %fusion.13 = bf16[1024,64]{0,1:T(8,128)(2,1)S(1)} fusion(bf16[4096,64]{0,1:T(8,128)(2,1)S(1)} %convolution_convert_fusion.1, bf16[1024,4096]{1,0:T(8,128)(2,1)} %param.6), kind=kOutput, calls=%fused_computation.35 | convolution fusion | flops 536936448 | bytes 9043968 | tf_op jit(solution)/shard_map/dot_general | solution.py:52
  105.7 66.4 %all-reduce.8.cloned.1.call-done = f32[256,256]{1,0:T(8,128)} async-done(((f32[256,256]{1,0:T(8,128)}), f32[256,256]{1,0:T(8,128)}) %all-reduce.8.cloned.1.call-update) | async-done | bytes 262160 | tf_op jit(solution)/shard_map/psum | solution.py:76
  174.3 11.7 %cholesky.130 = f32[128,128]{1,0:T(8,128)S(1)} custom-call(f32[128,128]{1,0:T(8,128)S(1)} %cholesky.194), custom_call_target="Cholesky" | custom-call | tf_op jit(solution)/shard_map/jit(cholesky)/cholesky | solution.py:77
  186.1 9.8 %custom-call.13 = f32[1,128,128]{1,2,0:T(8,128)S(1)} custom-call(f32[1,128,128]{2,1,0:T(8,128)S(1)} %get-tuple-element.54), custom_call_target="InvertDiagBlocksLowerTriangular" | custom-call | tf_op jit(solution)/shard_map/jit(cholesky)/cholesky | solution.py:77
  196.4 11.9 %cholesky.147 = f32[128,128]{1,0:T(8,128)S(1)} custom-call(f32[128,128]{1,0:T(8,128)S(1)} %convolution_subtract_fusion.6), custom_call_target="Cholesky" | custom-call | tf_op jit(solution)/shard_map/jit(cholesky)/cholesky | solution.py:77
  211.1 4.1 while.4
  211.8 1.4 bitcast_dynamic-update-slice_fusion.4
  213.9 1.4 bitcast_dynamic-update-slice_fusion.4
  215.3 19.7 %custom-call.14 = f32[2,128,128]{1,2,0:T(8,128)S(1)} custom-call(f32[2,128,128]{2,1,0:T(8,128)S(1)} %get-tuple-element.21), custom_call_target="InvertDiagBlocksLowerTriangular" | custom-call | tf_op jit(solution)/shard_map/jit(_solve_triangular)/triangular_solve | solution.py:23
  235.0 3.6 fusion.5
  238.6 1.9 convolution_subtract_fusion.1
  240.6 1.9 fusion.42
  244.7 41.0 %all-gather.9.cloned.1.call-done = bf16[1280,512]{0,1:T(8,128)(2,1)} async-done(((bf16[1280,64]{0,1:T(8,128)(2,1)}), bf16[1280,512]{0,1:T(8,128)(2,1)}) %all-gather.9.cloned.1.call-update) | async-done | bytes 1310736 | tf_op jit(solution)/shard_map/all_gather | solution.py:60
  285.7 1.7 convolution_convert_fusion.2
  287.5 5.1 %convolution_subtract_fusion.3 = f32[64,4096]{1,0:T(8,128)S(1)} fusion(bf16[1024,4096]{1,0:T(8,128)(2,1)} %param.6, bf16[2,64,4096]{2,1,0:T(8,128)(2,1)S(1)} %copy-done.7, bf16[1280,64]{0,1:T(8,128)(2,1)S(1)} %convolution_convert_fusion.2), kind=kOutput, calls=%fused_computation.11 | convolution fusion | flops 537395200 | bytes 10092544 | tf_op jit(solution)/shard_map/dot_general | solution.py:17
  293.2 1.7 fusion.16
  295.6 31.2 %all-reduce.10.cloned.1.call-done = f32[256,256]{1,0:T(8,128)} async-done(((f32[256,256]{1,0:T(8,128)}), f32[256,256]{1,0:T(8,128)}) %all-reduce.10.cloned.1.call-update) | async-done | bytes 262160 | tf_op jit(solution)/shard_map/psum | solution.py:76
  327.8 73.5 %all-reduce.12.cloned.1.call-done = f32[256,256]{1,0:T(8,128)} async-done(((f32[256,256]{1,0:T(8,128)}), f32[256,256]{1,0:T(8,128)}) %all-reduce.12.cloned.1.call-update) | async-done | bytes 262160 | tf_op jit(solution)/shard_map/psum | solution.py:76
  403.7 11.7 %cholesky.164 = f32[128,128]{1,0:T(8,128)S(1)} custom-call(f32[128,128]{1,0:T(8,128)S(1)} %cholesky.197), custom_call_target="Cholesky" | custom-call | tf_op jit(solution)/shard_map/jit(cholesky)/cholesky | solution.py:77
  415.4 9.8 %custom-call.15 = f32[1,128,128]{1,2,0:T(8,128)S(1)} custom-call(f32[1,128,128]{2,1,0:T(8,128)S(1)} %get-tuple-element.50), custom_call_target="InvertDiagBlocksLowerTriangular" | custom-call | tf_op jit(solution)/shard_map/jit(cholesky)/cholesky | solution.py:77
  425.7 11.7 %cholesky.181 = f32[128,128]{1,0:T(8,128)S(1)} custom-call(f32[128,128]{1,0:T(8,128)S(1)} %convolution_subtract_fusion.5), custom_call_target="Cholesky" | custom-call | tf_op jit(solution)/shard_map/jit(cholesky)/cholesky | solution.py:77
  440.1 4.1 while.5
  444.2 19.7 %custom-call.16 = f32[2,128,128]{1,2,0:T(8,128)S(1)} custom-call(f32[2,128,128]{2,1,0:T(8,128)S(1)} %get-tuple-element.22), custom_call_target="InvertDiagBlocksLowerTriangular" | custom-call | tf_op jit(solution)/shard_map/jit(_solve_triangular)/triangular_solve | solution.py:23
  464.0 3.6 fusion.3
  467.6 1.9 convolution_subtract_fusion
  469.6 1.9 fusion.38
  471.7 1.5 pad_maximum_fusion.1
  (96 shorter events, 22.2 us)
Async XLA Ops:
  6.5 51.7 %all-gather.5.cloned.1.call-start = ((), (), s32[]{:S(2)}) async-start(), calls=%async_computation | async-start | bytes 1179648 | tf_op jit(solution)/shard_map/all_gather | solution.py:60
  7.5 50.7 %copy-start.6 = (bf16[2,64,4096]{2,1,0:T(8,128)(2,1)S(1)}, bf16[2,64,4096]{2,1,0:T(8,128)(2,1)}, u32[]{:S(2)}) copy-start(bf16[2,64,4096]{2,1,0:T(8,128)(2,1)} %param.7) | copy-start | bytes 3145732
  15.0 82.6 %all-reduce.6.cloned.1.call-start = ((), (), s32[]{:S(2)}) async-start(), calls=%async_computation.1 | async-start | bytes 524288 | tf_op jit(solution)/shard_map/psum | solution.py:76
  64.1 33.7 %copy-start.5 = (f32[64,4096]{1,0:T(8,128)}, f32[64,4096]{1,0:T(8,128)S(1)}, u32[]{:S(2)}) copy-start(f32[64,4096]{1,0:T(8,128)S(1)} %convolution_subtract_fusion.4) | copy-start | bytes 3145732
  65.8 0.7 copy-start.8
  66.5 105.6 %all-reduce.8.cloned.1.call-start = ((), (), s32[]{:S(2)}) async-start(), calls=%async_computation.2 | async-start | bytes 524288 | tf_op jit(solution)/shard_map/psum | solution.py:76
  97.7 137.3 %all-gather.7.cloned.1.call-start = ((), (), s32[]{:S(2)}) async-start(), calls=%async_computation.3 | async-start | bytes 5242880 | tf_op jit(solution)/shard_map/all_gather | solution.py:78
  98.2 187.5 %all-gather.9.cloned.1.call-start = ((), (), s32[]{:S(2)}) async-start(), calls=%async_computation.4 | async-start | bytes 1474560 | tf_op jit(solution)/shard_map/all_gather | solution.py:60
  235.0 3.7 copy-start.2
  242.5 1.3 copy-start
  243.8 43.6 %copy-start.7 = (bf16[2,64,4096]{2,1,0:T(8,128)(2,1)S(1)}, bf16[2,64,4096]{2,1,0:T(8,128)(2,1)}, u32[]{:S(2)}) copy-start(bf16[2,64,4096]{2,1,0:T(8,128)(2,1)} %param.7) | copy-start | bytes 3145732
  244.6 82.3 %all-reduce.10.cloned.1.call-start = ((), (), s32[]{:S(2)}) async-start(), calls=%async_computation.5 | async-start | bytes 524288 | tf_op jit(solution)/shard_map/psum | solution.py:76
  287.5 5.2 %copy-start.1 = (f32[128,4096]{1,0:T(8,128)S(1)}, f32[128,4096]{1,0:T(8,128)}, u32[]{:S(2)}) copy-start(f32[128,4096]{1,0:T(8,128)} %copy-done) | copy-start | bytes 6291460
  293.1 34.2 %copy-start.4 = (f32[64,4096]{1,0:T(8,128)}, f32[64,4096]{1,0:T(8,128)S(1)}, u32[]{:S(2)}) copy-start(f32[64,4096]{1,0:T(8,128)S(1)} %convolution_subtract_fusion.2) | copy-start | bytes 3145732
  294.8 0.7 copy-start.9
  295.6 105.7 %all-reduce.12.cloned.1.call-start = ((), (), s32[]{:S(2)}) async-start(), calls=%async_computation.6 | async-start | bytes 524288 | tf_op jit(solution)/shard_map/psum | solution.py:76
  326.8 137.1 %all-gather.11.cloned.1.call-start = ((), (), s32[]{:S(2)}) async-start(), calls=%async_computation.7 | async-start | bytes 5242880 | tf_op jit(solution)/shard_map/all_gather | solution.py:78
  464.0 3.7 copy-start.3
Sparse Core Ops, SparseCore 0:
  15.2 42.9 all-gather.4
  66.6 30.9 all-reduce.5
  101.0 71.0 all-reduce.7
  173.5 33.7 all-gather.6
  244.7 41.0 all-gather.8
  295.7 31.1 all-reduce.9
  330.2 71.0 all-reduce.11
  402.8 33.7 all-gather.10
